TPU v7x, 32 devices: a whole 2x2x4 slice. The times are simulated.
32 devices in a mesh: hist: 16 (over z, x, core), orb: 2 (over y).
Axes of the slice: x: 2, y: 2, z: 4, core: 2. Of those that a mesh axis runs over, the one named last changes fastest.
Arguments:
- g_hist: bfloat16 [32, 64, 2048], P('hist', 'orb'), may hold values from -6 to 6
- sigma_hist: bfloat16 [2, 64, 2048], P(None, None, 'hist'), may hold values from -0.125 to 0.125
- diag_inv: float32 [32, 64, 64], P('hist'), may hold values from -0.75 to 0.75
- previous: float32 [2, 32, 64, 64], P(None, 'hist', 'orb'), may hold values from -6 to 6
- block_of_slot: int32 [16], replicated, may hold values from 0 to 15, each once
- front_pos: int32 [2], replicated, may hold values from 16 to 31
Outputs:
- g_row: float32 [2, 32, 64, 64], P(None, 'hist', 'orb')
- sigma_row: float32 [2, 32, 64, 64], P(None, 'hist', 'orb')
Inputs may be any that keep to these rules, and one draw needn't show every extreme that they name: `block_of_slot`: every block index appears once.
All inputs are finite; a program needn't handle non-finite values.
Results may differ from a plain program's by a relative error of at most 0.0003.
Values may be sent and summed in bfloat16 or wider, within the bound.
A program may use at most 64 MiB of HBM per device.

v0:
```python
import jax
import jax.numpy as jnp
from jax import lax
from jax.sharding import PartitionSpec as P

COUPLING = 0.5


def broadcast(value, axis, root):
    mine = lax.axis_index(axis) == root
    return lax.psum(jnp.where(mine, value, jnp.zeros_like(value)), axis)


def contract(g_piece, s_piece, times, col_time, front_pos):
    g_kept = jnp.where(
        (times[None, :] >= col_time[:, None])[:, None, :], g_piece, jnp.zeros_like(g_piece)
    )
    s_kept = jnp.where(
        (times[None, :] <= front_pos[:, None])[:, None, :], s_piece, jnp.zeros_like(s_piece)
    )
    return jnp.einsum("tcx,fax->ftca", g_kept, s_kept, preferred_element_type=jnp.float32)


def inverse_row(diag_inv, when, col_count):
    local = lax.dynamic_index_in_dim(diag_inv, when % col_count, 0, keepdims=False)
    return broadcast(local, "hist", when // col_count)


def body(g_hist, sigma_hist, diag_inv, previous, block_of_slot, front_pos):
    col_count = g_hist.shape[0]
    half_cols = g_hist.shape[1]
    orb_width = sigma_hist.shape[1]
    orb_id = lax.axis_index("orb")
    slot_id = lax.axis_index("hist")
    my_block = lax.dynamic_index_in_dim(block_of_slot, slot_id, 0, keepdims=False)
    col_time = my_block * col_count + jnp.arange(col_count, dtype=jnp.int32)
    piece = lax.all_gather(sigma_hist, "hist", axis=2, tiled=True)
    count = piece.shape[2]
    times = jnp.arange(count, dtype=jnp.int32) // orb_width
    integral = contract(g_hist, piece, times, col_time, front_pos)
    combined = previous + integral
    rows = jnp.stack([inverse_row(diag_inv, front_pos[front], col_count) for front in range(2)])
    g_row = jnp.einsum("ftcb,fab->ftca", combined, rows, precision=lax.Precision.HIGHEST)
    whole = lax.all_gather(g_row, "orb", axis=2, tiled=True)
    mirror = jnp.swapaxes(lax.dynamic_slice_in_dim(whole, orb_id * half_cols, half_cols, 3), 2, 3)
    sigma_row = COUPLING * g_row * g_row * mirror
    return (g_row, sigma_row)


def solution(mesh):
    in_specs = (
        P("hist", "orb", None),
        P(None, None, "hist"),
        P("hist", None, None),
        P(None, "hist", "orb", None),
        P(),
        P(),
    )
    out_specs = (P(None, "hist", "orb", None), P(None, "hist", "orb", None))
    return jax.shard_map(body, mesh=mesh, in_specs=in_specs, out_specs=out_specs, check_vma=False)
```

profile of v0, /device:TPU:0, one launch (start us, length us, event | category | flops | bytes accessed | tf_op | source)
XLA Modules:
  0.0 99.1 jit_solution(8734970899965628988)
XLA Ops:
  0.6 0.0 copy-start.4
  0.6 0.0 copy-start.3
  0.6 25.0 %all_gather.6 = bf16[2,64,2048]{2,1,0:T(8,128)(2,1)S(1)} all-gather(bf16[2,64,128]{2,1,0:T(8,128)(2,1)} %param.7), channel_id=1, replica_groups=mesh['hist'=16,'orb'=2] {'hist'}, dimensions={2}, use_global_device_ids=true | all-gather | bytes 557056 | tf_op jit(solution)/shard_map/all_gather | solution.py:37
  25.6 0.0 copy-start.5
  25.6 0.7 copy-done.5
  26.3 0.6 dynamic_slice.14
  27.5 0.0 copy-start.2
  27.5 0.6 copy-done.2
  28.2 0.1 broadcast_compare_fusion
  28.3 0.0 copy-done.4
  28.3 0.0 copy-done.3
  28.3 0.4 fusion
  28.7 0.0 copy-start.1
  28.7 0.6 fusion.18
  34.5 0.0 copy-done.1
  34.5 57.9 %all-reduce = (f32[1,64,64]{2,1,0:T(8,128)S(1)}, f32[1,64,64]{2,1,0:T(8,128)S(1)}) all-reduce(f32[1,64,64]{2,1,0:T(8,128)S(1)} %get-tuple-element.7, f32[1,64,64]{2,1,0:T(8,128)S(1)} %get-tuple-element.6), channel_id=1, replica_groups=mesh['hist'=16,'orb'=2] {'hist'}, use_global_device_ids=true, to_apply=%region_1.2 | all-reduce | flops 8192 | bytes 65536 | tf_op jit(solution)/shard_map/psum | solution.py:11
  92.4 0.2 fusion.10
  92.7 0.0 copy-start
  92.7 0.1 copy.8
  92.8 0.5 copy-done
  93.3 4.9 %all_gather.7 = f32[2,2,64,64]{3,2,1,0:T(8,128)S(1)} all-gather(f32[2,2,32,64]{3,2,1,0:T(8,128)S(1)} %fusion.10), channel_id=1, replica_groups=mesh['hist'=16,'orb'=2] {'orb'}, dimensions={2}, use_global_device_ids=true | all-gather | bytes 98304 | tf_op jit(solution)/shard_map/all_gather | solution.py:44
  98.2 0.1 fusion.8
  98.3 0.7 copy.10
  (3 shorter events, 0.0 us)
Async XLA Ops:
  0.6 27.6 %copy-start.4 = (f32[2,2,32,64]{3,2,1,0:T(8,128)S(1)}, f32[2,2,32,64]{3,2,1,0:T(8,128)}, u32[]{:S(2)}) copy-start(f32[2,2,32,64]{3,2,1,0:T(8,128)} %param.9) | copy-start | bytes 98308
  0.6 27.6 %copy-start.3 = (bf16[2,32,2048]{2,1,0:T(8,128)(2,1)S(1)}, bf16[2,32,2048]{2,1,0:T(8,128)(2,1)}, u32[]{:S(2)}) copy-start(bf16[2,32,2048]{2,1,0:T(8,128)(2,1)} %param.6) | copy-start | bytes 786436
  25.6 0.7 copy-start.5
  27.5 0.7 copy-start.2
  28.7 5.8 %copy-start.1 = (f32[2,64,64]{2,1,0:T(8,128)S(1)}, f32[2,64,64]{2,1,0:T(8,128)}, u32[]{:S(2)}) copy-start(f32[2,64,64]{2,1,0:T(8,128)} %param.8) | copy-start | bytes 98308
  92.7 0.6 copy-start
where the time goes:
time: 99.3 us; the launch traced here: 99.1 us
  blocking collectives  87.8 us (88%)
  between operations  6.62 us (7%)
  local copies, waits for them, and re-layouts  3.81 us (4%)
    psum x1, blocking collectives, broadcast(): return lax.psum(jnp.where(mine, value, jnp.zeros_like(value)), axis)  57.9 us
    all_gather x1, blocking collectives, body(): piece = lax.all_gather(sigma_hist, 'hist', axis=2, tiled=True)  25 us
    all_gather x1, blocking collectives, body(): whole = lax.all_gather(g_row, 'orb', axis=2, tiled=True)  4.92 us
    unnamed x13, local copies, waits for them, and re-layouts  2.55 us

commit v1 on v0

--- a/solution.py
+++ b/solution.py
@@ -34,7 +34,14 @@
     slot_id = lax.axis_index("hist")
     my_block = lax.dynamic_index_in_dim(block_of_slot, slot_id, 0, keepdims=False)
     col_time = my_block * col_count + jnp.arange(col_count, dtype=jnp.int32)
-    piece = lax.all_gather(sigma_hist, "hist", axis=2, tiled=True)
+    size = lax.axis_size("hist")
+    right = [(i, (i + 1) % size) for i in range(size)]
+    shards = [sigma_hist]
+    for far in range(1, size):
+        shards = [lax.ppermute(shards[0], "hist", right), *shards]
+    full = jnp.concatenate(shards, axis=2)
+    shift = (lax.axis_index("hist") + 1) * shards[-1].shape[2]
+    piece = jnp.roll(full, shift, axis=2)
     count = piece.shape[2]
     times = jnp.arange(count, dtype=jnp.int32) // orb_width
     integral = contract(g_hist, piece, times, col_time, front_pos)

time: 99.3 us -> 158 us (1.59)
  waiting for transfers between devices: 0 us -> 77.4 us
  blocking collectives: 87.8 us -> 67 us
    ppermute x0 -> x15, waiting for transfers between devices: none -> 77.4 us  [body(): shards = [lax.ppermute(shards[0], 'hist', right), *shards]]
    all_gather x1 -> x0, blocking collectives: 25 us -> none  [body(): piece = lax.all_gather(sigma_hist, 'hist', axis=2, tiled=True)]
    psum x1, blocking collectives: 57.9 us -> 62 us  [broadcast(): return lax.psum(jnp.where(mine, value, jnp.zeros_like(value)), axis)]
    unnamed x13 -> x46, local copies, waits for them, and re-layouts: 2.55 us -> 3.36 us
  transfers between devices with their start and end apart: 0 -> 15, of which waited for: 0 -> 14; matrix products, arithmetic and copies ran while one was open for 0% -> 1% of each run, Pallas kernels for 0% -> 0%
where the time goes in v1:
time: 158 us; the launch traced here: 157 us
  waiting for transfers between devices  77.4 us (49%)
  blocking collectives  67 us (42%)
  between operations  6.8 us (4%)
  local copies, waits for them, and re-layouts  4.63 us (3%)
    ppermute x15, waiting for transfers between devices, body(): shards = [lax.ppermute(shards[0], 'hist', right), *shards]  77.4 us
    psum x1, blocking collectives, broadcast(): return lax.psum(jnp.where(mine, value, jnp.zeros_like(value)), axis)  62 us
    all_gather x1, blocking collectives, body(): whole = lax.all_gather(g_row, 'orb', axis=2, tiled=True)  4.93 us
    unnamed x46, local copies, waits for them, and re-layouts  3.36 us
  transfers between devices with their start and end apart: 15, of which 14 were waited for; matrix products, arithmetic and copies ran while one was open for 1% of the time, Pallas kernels for 0%

profile of v1, /device:TPU:0, one launch (start us, length us, event | category | flops | bytes accessed | tf_op | source)
XLA Modules:
  0.0 157.2 jit_solution(4675046525050747533)
XLA Ops:
  0.6 0.5 collective-permute-start
  1.2 6.8 %collective-permute-done = bf16[2,64,128]{2,1,0:T(8,128)(2,1)S(1)} collective-permute-done((bf16[2,64,128]{2,1,0:T(8,128)(2,1)}, bf16[2,64,128]{2,1,0:T(8,128)(2,1)S(1)}, u32[]{:S(2)}, u32[]{:S(2)}) %collective-permute-start) | collective-permute-done | bytes 32800 | tf_op jit(solution)/shard_map/ppermute | solution.py:41
  7.9 6.0 %collective-permute-done.1 = bf16[2,64,128]{2,1,0:T(8,128)(2,1)S(1)} collective-permute-done((bf16[2,64,128]{2,1,0:T(8,128)(2,1)S(1)}, bf16[2,64,128]{2,1,0:T(8,128)(2,1)S(1)}, u32[]{:S(2)}, u32[]{:S(2)}) %collective-permute-start.1) | collective-permute-done | bytes 32800 | tf_op jit(solution)/shard_map/ppermute | solution.py:41
  14.0 6.0 %collective-permute-done.2 = bf16[2,64,128]{2,1,0:T(8,128)(2,1)S(1)} collective-permute-done((bf16[2,64,128]{2,1,0:T(8,128)(2,1)S(1)}, bf16[2,64,128]{2,1,0:T(8,128)(2,1)S(1)}, u32[]{:S(2)}, u32[]{:S(2)}) %collective-permute-start.2) | collective-permute-done | bytes 32800 | tf_op jit(solution)/shard_map/ppermute | solution.py:41
  20.0 6.0 %collective-permute-done.3 = bf16[2,64,128]{2,1,0:T(8,128)(2,1)S(1)} collective-permute-done((bf16[2,64,128]{2,1,0:T(8,128)(2,1)S(1)}, bf16[2,64,128]{2,1,0:T(8,128)(2,1)S(1)}, u32[]{:S(2)}, u32[]{:S(2)}) %collective-permute-start.3) | collective-permute-done | bytes 32800 | tf_op jit(solution)/shard_map/ppermute | solution.py:41
  26.1 6.0 %collective-permute-done.4 = bf16[2,64,128]{2,1,0:T(8,128)(2,1)S(1)} collective-permute-done((bf16[2,64,128]{2,1,0:T(8,128)(2,1)S(1)}, bf16[2,64,128]{2,1,0:T(8,128)(2,1)S(1)}, u32[]{:S(2)}, u32[]{:S(2)}) %collective-permute-start.4) | collective-permute-done | bytes 32800 | tf_op jit(solution)/shard_map/ppermute | solution.py:41
  32.1 6.0 %collective-permute-done.5 = bf16[2,64,128]{2,1,0:T(8,128)(2,1)S(1)} collective-permute-done((bf16[2,64,128]{2,1,0:T(8,128)(2,1)S(1)}, bf16[2,64,128]{2,1,0:T(8,128)(2,1)S(1)}, u32[]{:S(2)}, u32[]{:S(2)}) %collective-permute-start.5) | collective-permute-done | bytes 32800 | tf_op jit(solution)/shard_map/ppermute | solution.py:41
  38.1 6.0 %collective-permute-done.6 = bf16[2,64,128]{2,1,0:T(8,128)(2,1)S(1)} collective-permute-done((bf16[2,64,128]{2,1,0:T(8,128)(2,1)S(1)}, bf16[2,64,128]{2,1,0:T(8,128)(2,1)S(1)}, u32[]{:S(2)}, u32[]{:S(2)}) %collective-permute-start.6) | collective-permute-done | bytes 32800 | tf_op jit(solution)/shard_map/ppermute | solution.py:41
  44.2 6.0 %collective-permute-done.7 = bf16[2,64,128]{2,1,0:T(8,128)(2,1)S(1)} collective-permute-done((bf16[2,64,128]{2,1,0:T(8,128)(2,1)S(1)}, bf16[2,64,128]{2,1,0:T(8,128)(2,1)S(1)}, u32[]{:S(2)}, u32[]{:S(2)}) %collective-permute-start.7) | collective-permute-done | bytes 32800 | tf_op jit(solution)/shard_map/ppermute | solution.py:41
  50.2 6.0 %collective-permute-done.8 = bf16[2,64,128]{2,1,0:T(8,128)(2,1)S(1)} collective-permute-done((bf16[2,64,128]{2,1,0:T(8,128)(2,1)S(1)}, bf16[2,64,128]{2,1,0:T(8,128)(2,1)S(1)}, u32[]{:S(2)}, u32[]{:S(2)}) %collective-permute-start.8) | collective-permute-done | bytes 32800 | tf_op jit(solution)/shard_map/ppermute | solution.py:41
  56.2 6.0 %collective-permute-done.9 = bf16[2,64,128]{2,1,0:T(8,128)(2,1)S(1)} collective-permute-done((bf16[2,64,128]{2,1,0:T(8,128)(2,1)S(1)}, bf16[2,64,128]{2,1,0:T(8,128)(2,1)S(1)}, u32[]{:S(2)}, u32[]{:S(2)}) %collective-permute-start.9) | collective-permute-done | bytes 32800 | tf_op jit(solution)/shard_map/ppermute | solution.py:41
  62.3 0.7 copy-done.6
  62.9 0.6 dynamic_slice.19
  64.2 4.1 %collective-permute-done.10 = bf16[2,64,128]{2,1,0:T(8,128)(2,1)S(1)} collective-permute-done((bf16[2,64,128]{2,1,0:T(8,128)(2,1)S(1)}, bf16[2,64,128]{2,1,0:T(8,128)(2,1)S(1)}, u32[]{:S(2)}, u32[]{:S(2)}) %collective-permute-start.10) | collective-permute-done | bytes 32800 | tf_op jit(solution)/shard_map/ppermute | solution.py:41
  68.3 6.0 %collective-permute-done.11 = bf16[2,64,128]{2,1,0:T(8,128)(2,1)S(1)} collective-permute-done((bf16[2,64,128]{2,1,0:T(8,128)(2,1)S(1)}, bf16[2,64,128]{2,1,0:T(8,128)(2,1)S(1)}, u32[]{:S(2)}, u32[]{:S(2)}) %collective-permute-start.11) | collective-permute-done | bytes 32800 | tf_op jit(solution)/shard_map/ppermute | solution.py:41
  74.4 0.1 broadcast_compare_fusion
  74.4 5.9 %collective-permute-done.12 = bf16[2,64,128]{2,1,0:T(8,128)(2,1)S(1)} collective-permute-done((bf16[2,64,128]{2,1,0:T(8,128)(2,1)S(1)}, bf16[2,64,128]{2,1,0:T(8,128)(2,1)S(1)}, u32[]{:S(2)}, u32[]{:S(2)}) %collective-permute-start.12) | collective-permute-done | bytes 32800 | tf_op jit(solution)/shard_map/ppermute | solution.py:41
  80.4 0.6 fusion.20
  86.2 0.2 collective-permute-done.13
  86.5 62.0 %all-reduce = (f32[1,64,64]{2,1,0:T(8,128)S(1)}, f32[1,64,64]{2,1,0:T(8,128)S(1)}) all-reduce(f32[1,64,64]{2,1,0:T(8,128)S(1)} %get-tuple-element.7, f32[1,64,64]{2,1,0:T(8,128)S(1)} %get-tuple-element.6), channel_id=1, replica_groups=mesh['hist'=16,'orb'=2] {'hist'}, use_global_device_ids=true, to_apply=%region_1.2 | all-reduce | flops 8192 | bytes 65536 | tf_op jit(solution)/shard_map/psum | solution.py:11
  148.8 0.0 copy-start.1
  148.8 0.7 copy-done.1
  149.7 0.0 copy-start.4
  149.8 0.0 copy-start.5
  149.9 0.8 copy-done.4
  150.7 0.0 copy-done.5
  150.7 0.4 fusion
  151.1 0.2 fusion.11
  151.3 4.9 %all_gather.3 = f32[2,2,64,64]{3,2,1,0:T(8,128)S(1)} all-gather(f32[2,2,32,64]{3,2,1,0:T(8,128)S(1)} %fusion.11), channel_id=1, replica_groups=mesh['hist'=16,'orb'=2] {'orb'}, dimensions={2}, use_global_device_ids=true | all-gather | bytes 98304 | tf_op jit(solution)/shard_map/all_gather | solution.py:51
  156.3 0.1 copy.8
  156.4 0.1 fusion.9
  156.5 0.7 copy.10
  (57 shorter events, 0.5 us)
Async XLA Ops:
  0.6 7.3 %collective-permute-start = (bf16[2,64,128]{2,1,0:T(8,128)(2,1)}, bf16[2,64,128]{2,1,0:T(8,128)(2,1)S(1)}, u32[]{:S(2)}, u32[]{:S(2)}) collective-permute-start(bf16[2,64,128]{2,1,0:T(8,128)(2,1)} %param.7), channel_id=1, source_target_pairs={{0,2},{2,4},{4,6},{6,8},{8,10},{10,12},{12,14},{14,16},{16,18},{18... | collective-permute-start | bytes 98312 | tf_op jit(solution)/shard_map/ppermute | solution.py:41
  7.9 6.0 %collective-permute-start.1 = (bf16[2,64,128]{2,1,0:T(8,128)(2,1)S(1)}, bf16[2,64,128]{2,1,0:T(8,128)(2,1)S(1)}, u32[]{:S(2)}, u32[]{:S(2)}) collective-permute-start(bf16[2,64,128]{2,1,0:T(8,128)(2,1)S(1)} %collective-permute-done), channel_id=1, source_target_pairs={{0,2},{2,4},{4,6},{6,8},{8,10},{10,12},{12,14},{14,16},{16,18},{18... | collective-permute-start | bytes 98312 | tf_op jit(solution)/shard_map/ppermute | solution.py:41
  14.0 6.0 %collective-permute-start.2 = (bf16[2,64,128]{2,1,0:T(8,128)(2,1)S(1)}, bf16[2,64,128]{2,1,0:T(8,128)(2,1)S(1)}, u32[]{:S(2)}, u32[]{:S(2)}) collective-permute-start(bf16[2,64,128]{2,1,0:T(8,128)(2,1)S(1)} %collective-permute-done.1), channel_id=1, source_target_pairs={{0,2},{2,4},{4,6},{6,8},{8,10},{10,12},{12,14},{14,16},{16,18},{18... | collective-permute-start | bytes 98312 | tf_op jit(solution)/shard_map/ppermute | solution.py:41
  20.0 6.0 %collective-permute-start.3 = (bf16[2,64,128]{2,1,0:T(8,128)(2,1)S(1)}, bf16[2,64,128]{2,1,0:T(8,128)(2,1)S(1)}, u32[]{:S(2)}, u32[]{:S(2)}) collective-permute-start(bf16[2,64,128]{2,1,0:T(8,128)(2,1)S(1)} %collective-permute-done.2), channel_id=1, source_target_pairs={{0,2},{2,4},{4,6},{6,8},{8,10},{10,12},{12,14},{14,16},{16,18},{18... | collective-permute-start | bytes 98312 | tf_op jit(solution)/shard_map/ppermute | solution.py:41
  26.1 6.0 %collective-permute-start.4 = (bf16[2,64,128]{2,1,0:T(8,128)(2,1)S(1)}, bf16[2,64,128]{2,1,0:T(8,128)(2,1)S(1)}, u32[]{:S(2)}, u32[]{:S(2)}) collective-permute-start(bf16[2,64,128]{2,1,0:T(8,128)(2,1)S(1)} %collective-permute-done.3), channel_id=1, source_target_pairs={{0,2},{2,4},{4,6},{6,8},{8,10},{10,12},{12,14},{14,16},{16,18},{18... | collective-permute-start | bytes 98312 | tf_op jit(solution)/shard_map/ppermute | solution.py:41
  32.1 6.0 %collective-permute-start.5 = (bf16[2,64,128]{2,1,0:T(8,128)(2,1)S(1)}, bf16[2,64,128]{2,1,0:T(8,128)(2,1)S(1)}, u32[]{:S(2)}, u32[]{:S(2)}) collective-permute-start(bf16[2,64,128]{2,1,0:T(8,128)(2,1)S(1)} %collective-permute-done.4), channel_id=1, source_target_pairs={{0,2},{2,4},{4,6},{6,8},{8,10},{10,12},{12,14},{14,16},{16,18},{18... | collective-permute-start | bytes 98312 | tf_op jit(solution)/shard_map/ppermute | solution.py:41
  38.1 6.0 %collective-permute-start.6 = (bf16[2,64,128]{2,1,0:T(8,128)(2,1)S(1)}, bf16[2,64,128]{2,1,0:T(8,128)(2,1)S(1)}, u32[]{:S(2)}, u32[]{:S(2)}) collective-permute-start(bf16[2,64,128]{2,1,0:T(8,128)(2,1)S(1)} %collective-permute-done.5), channel_id=1, source_target_pairs={{0,2},{2,4},{4,6},{6,8},{8,10},{10,12},{12,14},{14,16},{16,18},{18... | collective-permute-start | bytes 98312 | tf_op jit(solution)/shard_map/ppermute | solution.py:41
  44.2 6.0 %collective-permute-start.7 = (bf16[2,64,128]{2,1,0:T(8,128)(2,1)S(1)}, bf16[2,64,128]{2,1,0:T(8,128)(2,1)S(1)}, u32[]{:S(2)}, u32[]{:S(2)}) collective-permute-start(bf16[2,64,128]{2,1,0:T(8,128)(2,1)S(1)} %collective-permute-done.6), channel_id=1, source_target_pairs={{0,2},{2,4},{4,6},{6,8},{8,10},{10,12},{12,14},{14,16},{16,18},{18... | collective-permute-start | bytes 98312 | tf_op jit(solution)/shard_map/ppermute | solution.py:41
  50.2 6.0 %collective-permute-start.8 = (bf16[2,64,128]{2,1,0:T(8,128)(2,1)S(1)}, bf16[2,64,128]{2,1,0:T(8,128)(2,1)S(1)}, u32[]{:S(2)}, u32[]{:S(2)}) collective-permute-start(bf16[2,64,128]{2,1,0:T(8,128)(2,1)S(1)} %collective-permute-done.7), channel_id=1, source_target_pairs={{0,2},{2,4},{4,6},{6,8},{8,10},{10,12},{12,14},{14,16},{16,18},{18... | collective-permute-start | bytes 98312 | tf_op jit(solution)/shard_map/ppermute | solution.py:41
  56.2 6.0 %collective-permute-start.9 = (bf16[2,64,128]{2,1,0:T(8,128)(2,1)S(1)}, bf16[2,64,128]{2,1,0:T(8,128)(2,1)S(1)}, u32[]{:S(2)}, u32[]{:S(2)}) collective-permute-start(bf16[2,64,128]{2,1,0:T(8,128)(2,1)S(1)} %collective-permute-done.8), channel_id=1, source_target_pairs={{0,2},{2,4},{4,6},{6,8},{8,10},{10,12},{12,14},{14,16},{16,18},{18... | collective-permute-start | bytes 98312 | tf_op jit(solution)/shard_map/ppermute | solution.py:41
  62.3 6.0 %collective-permute-start.10 = (bf16[2,64,128]{2,1,0:T(8,128)(2,1)S(1)}, bf16[2,64,128]{2,1,0:T(8,128)(2,1)S(1)}, u32[]{:S(2)}, u32[]{:S(2)}) collective-permute-start(bf16[2,64,128]{2,1,0:T(8,128)(2,1)S(1)} %collective-permute-done.9), channel_id=1, source_target_pairs={{0,2},{2,4},{4,6},{6,8},{8,10},{10,12},{12,14},{14,16},{16,18},{18... | collective-permute-start | bytes 98312 | tf_op jit(solution)/shard_map/ppermute | solution.py:41
  62.3 0.7 copy-start.6
  62.9 11.4 %copy-start.3 = (s32[2]{0:T(128)S(1)}, s32[2]{0:T(128)}, u32[]{:S(2)}) copy-start(s32[2]{0:T(128)} %param.11) | copy-start | bytes 28
  63.5 22.9 %copy-start.2 = (f32[2,64,64]{2,1,0:T(8,128)S(1)}, f32[2,64,64]{2,1,0:T(8,128)}, u32[]{:S(2)}) copy-start(f32[2,64,64]{2,1,0:T(8,128)} %param.8) | copy-start | bytes 98308
  68.3 6.0 %collective-permute-start.11 = (bf16[2,64,128]{2,1,0:T(8,128)(2,1)S(1)}, bf16[2,64,128]{2,1,0:T(8,128)(2,1)S(1)}, u32[]{:S(2)}, u32[]{:S(2)}) collective-permute-start(bf16[2,64,128]{2,1,0:T(8,128)(2,1)S(1)} %collective-permute-done.10), channel_id=1, source_target_pairs={{0,2},{2,4},{4,6},{6,8},{8,10},{10,12},{12,14},{14,16},{16,18},{18... | collective-permute-start | bytes 98312 | tf_op jit(solution)/shard_map/ppermute | solution.py:41
  74.3 6.0 %collective-permute-start.12 = (bf16[2,64,128]{2,1,0:T(8,128)(2,1)S(1)}, bf16[2,64,128]{2,1,0:T(8,128)(2,1)S(1)}, u32[]{:S(2)}, u32[]{:S(2)}) collective-permute-start(bf16[2,64,128]{2,1,0:T(8,128)(2,1)S(1)} %collective-permute-done.11), channel_id=1, source_target_pairs={{0,2},{2,4},{4,6},{6,8},{8,10},{10,12},{12,14},{14,16},{16,18},{18... | collective-permute-start | bytes 98312 | tf_op jit(solution)/shard_map/ppermute | solution.py:41
  80.4 6.1 %collective-permute-start.13 = (bf16[2,64,128]{2,1,0:T(8,128)(2,1)S(1)}, bf16[2,64,128]{2,1,0:T(8,128)(2,1)S(1)}, u32[]{:S(2)}, u32[]{:S(2)}) collective-permute-start(bf16[2,64,128]{2,1,0:T(8,128)(2,1)S(1)} %collective-permute-done.12), channel_id=1, source_target_pairs={{0,2},{2,4},{4,6},{6,8},{8,10},{10,12},{12,14},{14,16},{16,18},{18... | collective-permute-start | bytes 98312 | tf_op jit(solution)/shard_map/ppermute | solution.py:41
  86.4 62.1 %collective-permute-start.14 = (bf16[2,64,128]{2,1,0:T(8,128)(2,1)S(1)}, bf16[2,64,128]{2,1,0:T(8,128)(2,1)S(1)}, u32[]{:S(2)}, u32[]{:S(2)}) collective-permute-start(bf16[2,64,128]{2,1,0:T(8,128)(2,1)S(1)} %collective-permute-done.13), channel_id=1, source_target_pairs={{0,2},{2,4},{4,6},{6,8},{8,10},{10,12},{12,14},{14,16},{16,18},{18... | collective-permute-start | bytes 98312 | tf_op jit(solution)/shard_map/ppermute | solution.py:41
  148.8 0.8 copy-start.1
  149.7 1.0 copy-start.4
  149.8 0.9 copy-start.5
  151.3 4.9 %copy-start = (f32[2,2,32,64]{3,2,1,0:T(8,128)}, f32[2,2,32,64]{3,2,1,0:T(8,128)S(1)}, u32[]{:S(2)}) copy-start(f32[2,2,32,64]{3,2,1,0:T(8,128)S(1)} %fusion.11) | copy-start | bytes 98308
